TPU v7x, 32 devices: a whole 2x2x4 slice. The times are simulated.
32 devices in a mesh: dp: 4 (over y, core), expert: 4 (over z), pipe: 2 (over x).
Axes of the slice: x: 2, y: 2, z: 4, core: 2. Of those that a mesh axis runs over, the one named last changes fastest.
Arguments:
- inputs: bfloat16 [512, 4096], P('expert'), may hold values from -6 to 6
- cotangents: bfloat16 [512, 4096], P('expert'), may hold values from -6 to 6
- routes: int32 [512, 2], P('expert'), may hold values from 0 to 3, all different within a row; in each aligned block of 128 rows (0 to 127, 128 to 255, ...) at most 128 rows name the same one
- gates: float32 [512, 2], P('expert'), may hold values from 0.1 to 1
- w_gate: bfloat16 [4, 4096, 7168], P('expert', None, ('dp', 'pipe')), may hold values from -0.09375 to 0.09375
- w_up: bfloat16 [4, 4096, 7168], P('expert', None, ('dp', 'pipe')), may hold values from -0.09375 to 0.09375
- w_down: bfloat16 [4, 7168, 4096], P('expert', ('dp', 'pipe')), may hold values from -0.09375 to 0.09375
- proj_in: bfloat16 [4096, 32], replicated, may hold values from -0.09375 to 0.09375
- proj_out: bfloat16 [4096, 64], replicated, may hold values from -0.09375 to 0.09375
- proj_hid_a: bfloat16 [7168, 32], P(('dp', 'pipe')), may hold values from -0.0625 to 0.0625
- proj_hid_b: bfloat16 [7168, 64], P(('dp', 'pipe')), may hold values from -0.0625 to 0.0625
- queries: bfloat16 [256, 6144], P(('dp', 'pipe')), may hold values from -0.078125 to 0.078125
Outputs:
- token_scores: float32 [512, 256], P('expert', ('dp', 'pipe'))
- query_totals: float32 [256], P(('dp', 'pipe'))
Inputs may be any that keep to these rules, and one draw needn't show every extreme that they name: `routes`: each row names two different experts. Among the 128 tokens of one index of expert (aligned blocks), no expert is named more than 128 times, and in some blocks one expert is named exactly 128 times.
All inputs are finite; a program needn't handle non-finite values.
Results may differ from a plain program's by a relative error of at most 0.0041.
Values may be sent and summed in bfloat16 or wider, within the bound.
No kernel may reach another device: no remote copies, remote signals or barrier semaphores. Data moves between devices by JAX's collectives and lax.ppermute only.
A program may use at most 128 MiB of HBM per device.

v0:
```python
import math

import jax
import jax.numpy as jnp
from jax import lax
from jax.sharding import PartitionSpec as P


def slot_matrix(route_rows, gate_rows, experts, capacity):
    count = route_rows.shape[0]
    flat = route_rows.reshape(-1)
    labels = jnp.arange(experts, dtype=jnp.int32)
    onehot = (flat[:, None] == labels[None, :]).astype(jnp.int32)
    earlier = jnp.cumsum(onehot, axis=0) - onehot
    position = jnp.sum(onehot * (labels[None, :] * capacity + earlier), axis=1)
    slot_ids = jnp.arange(experts * capacity, dtype=jnp.int32)
    table = (
        (position[None, :] == slot_ids[:, None])
        .astype(jnp.float32)
        .reshape(experts * capacity, count, 2)
    )
    picks = jnp.sum(table, axis=2)
    weighted = jnp.sum(table * gate_rows[None, :, :], axis=2)
    return (picks, weighted)


def send_back(scores):
    return lax.all_to_all(scores, "expert", split_axis=0, concat_axis=0, tiled=True)


def body(
    inputs,
    cotangents,
    routes,
    gates,
    w_gate,
    w_up,
    w_down,
    proj_in,
    proj_out,
    proj_hid_a,
    proj_hid_b,
    queries,
):
    experts = lax.axis_size("expert")
    count = inputs.shape[0]
    width = inputs.shape[1]
    capacity = 4 * count // experts
    query_count = queries.shape[0]
    gate_proj = w_gate[0]
    up_proj = w_up[0]
    down_proj = w_down[0]
    picks, weighted = slot_matrix(routes, gates, experts, capacity)
    pick_rows = picks.astype(jnp.bfloat16)
    columns = width // lax.axis_size(("dp", "pipe"))
    column_start = lax.axis_index(("dp", "pipe")) * columns
    part_in = lax.dynamic_slice_in_dim(inputs, column_start, columns, 1)
    part_back = lax.dynamic_slice_in_dim(cotangents, column_start, columns, 1)
    buffer_in = jnp.dot(pick_rows, part_in, preferred_element_type=jnp.float32).astype(jnp.bfloat16)
    buffer_back = jnp.dot(pick_rows, part_back, preferred_element_type=jnp.float32).astype(
        jnp.bfloat16
    )
    sent_in, sent_back = (
        lax.all_to_all(
            buffer_in.reshape(experts, capacity, columns),
            "expert",
            split_axis=0,
            concat_axis=0,
            tiled=True,
        ),
        lax.all_to_all(
            buffer_back.reshape(experts, capacity, columns),
            "expert",
            split_axis=0,
            concat_axis=0,
            tiled=True,
        ),
    )
    full_in, full_back = (
        lax.all_gather(sent_in, ("dp", "pipe"), axis=2, tiled=True),
        lax.all_gather(sent_back, ("dp", "pipe"), axis=2, tiled=True),
    )
    slot_in = full_in.reshape(-1, width)
    gate_pre = jnp.dot(slot_in, gate_proj, preferred_element_type=jnp.float32)
    up_pre = jnp.dot(slot_in, up_proj, preferred_element_type=jnp.float32)
    sigma = jax.nn.sigmoid(gate_pre)
    hidden = (gate_pre * sigma * up_pre).astype(jnp.bfloat16)
    a_part = jnp.dot(hidden, proj_hid_a, preferred_element_type=jnp.float32)
    slot_back = full_back.reshape(-1, width)
    gate_pre, up_pre, sigma, a_part = (gate_pre, up_pre, sigma, a_part)
    back = lax.dot_general(
        slot_back, down_proj, (((1,), (1,)), ((), ())), preferred_element_type=jnp.float32
    )
    d_up = (back * gate_pre * sigma).astype(jnp.bfloat16)
    d_gate = (back * up_pre * sigma * (1.0 + gate_pre * (1.0 - sigma))).astype(jnp.bfloat16)
    b_up_part = jnp.dot(d_up, proj_hid_b, preferred_element_type=jnp.float32)
    b_gate_part = jnp.dot(d_gate, proj_hid_b, preferred_element_type=jnp.float32)
    a_hidden, b_up, b_gate = lax.psum((a_part, b_up_part, b_gate_part), ("dp", "pipe"))
    a_input = jnp.dot(slot_in, proj_in, preferred_element_type=jnp.float32)
    b_output = jnp.dot(slot_back, proj_out, preferred_element_type=jnp.float32)
    height = slot_in.shape[0]
    sketch = jnp.concatenate(
        [
            (a_hidden[:, :, None] * b_output[:, None, :]).reshape(height, -1),
            (a_input[:, :, None] * b_up[:, None, :]).reshape(height, -1),
            (a_input[:, :, None] * b_gate[:, None, :]).reshape(height, -1),
        ],
        axis=1,
    ).astype(jnp.bfloat16)
    scores = lax.dot_general(
        sketch, queries, (((1,), (1,)), ((), ())), preferred_element_type=jnp.float32
    )
    returned = send_back(scores.reshape(experts, capacity, query_count))
    token_scores = lax.dot_general(
        weighted,
        returned.reshape(-1, query_count),
        (((0,), (0,)), ((), ())),
        precision=lax.Precision.HIGHEST,
        preferred_element_type=jnp.float32,
    )
    scale = 1.0 / math.sqrt(count * experts)
    partial_sum = jnp.sum(token_scores, axis=0)
    totals = lax.psum(partial_sum, "expert")
    return (token_scores, totals * scale)


def solution(mesh):
    placed = (
        P("expert", None),
        P("expert", None),
        P("expert", None),
        P("expert", None),
        P("expert", None, ("dp", "pipe")),
        P("expert", None, ("dp", "pipe")),
        P("expert", ("dp", "pipe"), None),
        P(),
        P(),
        P(("dp", "pipe"), None),
        P(("dp", "pipe"), None),
        P(("dp", "pipe"), None),
    )
    return jax.shard_map(
        body,
        mesh=mesh,
        in_specs=placed,
        out_specs=(P("expert", ("dp", "pipe")), P(("dp", "pipe"))),
        check_vma=False,
    )
```

profile of v0, /device:TPU:0, one launch (start us, length us, event | category | flops | bytes accessed | tf_op | source)
XLA Modules:
  0.0 218.4 jit_solution(5094420722675360818)
XLA Ops:
  7.2 0.9 copy.40
  8.1 0.1 eq.45
  8.2 0.1 eq.41
  8.4 1.2 reduce-window.6
  9.6 0.1 slice.8
  9.7 0.1 copy.42
  9.9 0.1 copy.43
  9.9 0.1 add_bitcast_fusion
  10.0 0.1 fusion.28
  10.1 0.1 eq.49
  10.3 0.8 convert_reduce_fusion
  11.2 0.3 convolution_convert_fusion
  11.5 20.9 %all_to_all.15 = bf16[4,128,512]{2,1,0:T(8,128)(2,1)} all-to-all(bf16[4,128,512]{2,1,0:T(8,128)(2,1)S(1)} %bitcast.76), channel_id=1, replica_groups=mesh['dp'=4,'expert'=4,'pipe'=2] {'expert'}, dimensions={0} | all-to-all | bytes 1048576 | tf_op jit(solution)/shard_map/all_to_all | solution.py:71
  32.4 1.2 convolution_convert_fusion.1
  33.6 16.8 %all_to_all.16 = bf16[4,128,512]{2,1,0:T(8,128)(2,1)} all-to-all(bf16[4,128,512]{2,1,0:T(8,128)(2,1)S(1)} %bitcast.75), channel_id=1, replica_groups=mesh['dp'=4,'expert'=4,'pipe'=2] {'expert'}, dimensions={0} | all-to-all | bytes 1048576 | tf_op jit(solution)/shard_map/all_to_all | solution.py:64
  50.5 18.5 %all-gather.5.cloned.1.call-done = bf16[4,128,4096]{2,1,0:T(8,128)(2,1)} async-done(((bf16[4,128,512]{2,1,0:T(8,128)(2,1)}), bf16[4,128,4096]{2,1,0:T(8,128)(2,1)}) %all-gather.5.cloned.1.call-update) | async-done | bytes 4194320 | tf_op jit(solution)/shard_map/all_gather | solution.py:81
  69.0 3.7 %fusion.36 = f32[512,64]{0,1:T(8,128)S(1)} fusion(bf16[512,4096]{1,0:T(8,128)(2,1)} %bitcast.67, bf16[4096,64]{0,1:T(8,128)(2,1)S(1)} %copy-done.3), kind=kOutput, calls=%fused_computation.53 | convolution fusion | flops 268435456 | bytes 4849664 | tf_op jit(solution)/shard_map/dot_general | solution.py:100
  72.7 8.6 %fusion = f32[512,896]{1,0:T(8,128)S(1)} fusion(bf16[512,4096]{1,0:T(8,128)(2,1)S(1)} %bitcast.68, bf16[1,896,4096]{2,1,0:T(8,128)(2,1)} %param.18), kind=kOutput, calls=%fused_computation | convolution fusion | flops 3758096384 | bytes 13369344 | tf_op jit(solution)/shard_map/dot_general | solution.py:91
  81.3 26.9 %all-gather.3.cloned.1.call-done = bf16[4,128,4096]{2,1,0:T(8,128)(2,1)} async-done(((bf16[4,128,512]{2,1,0:T(8,128)(2,1)}), bf16[4,128,4096]{2,1,0:T(8,128)(2,1)}) %all-gather.3.cloned.1.call-update) | async-done | bytes 4194320 | tf_op jit(solution)/shard_map/all_gather | solution.py:80
  108.2 10.5 %fusion.4 = f32[512,896]{1,0:T(8,128)S(1)} fusion(bf16[512,4096]{1,0:T(8,128)(2,1)} %bitcast.69, bf16[1,4096,896]{2,1,0:T(8,128)(2,1)} %param.16), kind=kOutput, calls=%fused_computation.4 | convolution fusion | flops 3758096384 | bytes 13369344 | tf_op jit(solution)/shard_map/dot_general | solution.py:84
  118.8 8.7 %fusion.2 = f32[512,896]{1,0:T(8,128)S(1)} fusion(bf16[512,4096]{1,0:T(8,128)(2,1)S(1)} %bitcast.71, bf16[1,4096,896]{2,1,0:T(8,128)(2,1)} %param.17), kind=kOutput, calls=%fused_computation.2 | convolution fusion | flops 3758096384 | bytes 13369344 | tf_op jit(solution)/shard_map/dot_general | solution.py:85
  127.5 1.3 fusion.15
  128.8 1.5 fusion.17
  130.3 1.2 fusion.16
  131.6 3.5 %fusion.37 = f32[512,32]{0,1:T(8,128)S(1)} fusion(bf16[512,4096]{1,0:T(8,128)(2,1)} %bitcast.70, bf16[4096,32]{0,1:T(8,128)(2,1)S(1)} %copy-done.4), kind=kOutput, calls=%fused_computation.54 | convolution fusion | flops 134217728 | bytes 4521984 | tf_op jit(solution)/shard_map/dot_general | solution.py:99
  135.2 51.3 %all-reduce.3.cloned.1.call-done = (f32[512,64]{0,1:T(8,128)}, f32[512,64]{0,1:T(8,128)}, f32[512,32]{0,1:T(8,128)}) async-done(((f32[512,64]{0,1:T(8,128)}, f32[512,64]{0,1:T(8,128)}, f32[512,32]{0,1:T(8,128)}), (f32[512,64]{0,1:T(8,128)}, f32[512,64]{0,1:T(8,128)}, f32[512,32]{0,1:T(8,128)})) %all-reduce.3.cloned.1.call-update) | async-done | bytes 327696 | tf_op jit(solution)/shard_map/psum | solution.py:98
  186.4 3.1 %multiply_convert_fusion.1 = (bf16[512,32,64]{0,2,1:T(8,128)(2,1)S(1)}, bf16[512,32,64]{0,2,1:T(8,128)(2,1)S(1)}, bf16[512,32,64]{0,2,1:T(8,128)(2,1)S(1)}) fusion(f32[512,64]{0,1:T(8,128)} %get-tuple-element.5, f32[512,32]{0,1:T(8,128)S(1)} %fusion.37, f32[512,64]{0,1:T(8,128)} %get-tuple-element.4, f32[512,64]{0,1:T(8,128)S(1)} %fusion.36, ...), kind=kLoop, calls=%fused_computation.13 | loop fusion | flops 6291456 | bytes 6815744 | tf_op jit(solution)/shard_map/convert.4
  189.6 1.3 fusion.12
  190.9 10.1 %all_to_all.17 = f32[4,128,32]{1,2,0:T(8,128)S(1)} all-to-all(f32[4,128,32]{1,2,0:T(8,128)S(1)} %bitcast.77), channel_id=1, replica_groups=mesh['dp'=4,'expert'=4,'pipe'=2] {'expert'}, dimensions={0} | all-to-all | bytes 131072 | tf_op jit(solution)/shard_map/all_to_all | solution.py:28
  201.1 1.0 fusion.35
  202.1 9.3 %psum.31 = f32[32]{0:T(128)S(1)} all-reduce(f32[32]{0:T(128)S(1)} %get-tuple-element.9), channel_id=1, replica_groups=mesh['dp'=4,'expert'=4,'pipe'=2] {'expert'}, use_global_device_ids=true, to_apply=%region_9.10 | all-reduce | flops 32 | bytes 256 | tf_op jit(solution)/shard_map/psum | solution.py:123
  211.3 0.5 broadcast_multiply_fusion
  (28 shorter events, 0.3 us)
Async XLA Ops:
  7.2 4.0 %copy-start = (bf16[128,4096]{1,0:T(8,128)(2,1)S(1)}, bf16[128,4096]{1,0:T(8,128)(2,1)}, u32[]{:S(2)}) copy-start(bf16[128,4096]{1,0:T(8,128)(2,1)} %param.13) | copy-start | bytes 3145732
  7.2 61.8 %all-gather.5.cloned.1.call-start = ((), (), s32[]{:S(2)}) async-start(), calls=%async_computation.4 | async-start | bytes 4718592 | tf_op jit(solution)/shard_map/all_gather | solution.py:81
  11.5 57.5 %copy-start.3 = (bf16[4096,64]{0,1:T(8,128)(2,1)S(1)}, bf16[4096,64]{0,1:T(8,128)(2,1)}, u32[]{:S(2)}) copy-start(bf16[4096,64]{0,1:T(8,128)(2,1)} %param.20) | copy-start | bytes 1572868
  32.4 75.9 %all-gather.3.cloned.1.call-start = ((), (), s32[]{:S(2)}) async-start(), calls=%async_computation.3 | async-start | bytes 4718592 | tf_op jit(solution)/shard_map/all_gather | solution.py:80
  50.4 136.0 %all-reduce.3.cloned.1.call-start = ((), (), s32[]{:S(2)}) async-start(), calls=%async_computation.5 | async-start | bytes 655360 | tf_op jit(solution)/shard_map/psum | solution.py:98
  69.0 3.7 %copy-start.1 = (bf16[4,128,4096]{2,1,0:T(8,128)(2,1)S(1)}, bf16[4,128,4096]{2,1,0:T(8,128)(2,1)}, u32[]{:S(2)}) copy-start(bf16[4,128,4096]{2,1,0:T(8,128)(2,1)} %all-gather.5.cloned.1.call-done) | copy-start | bytes 12582916
  108.2 10.5 %copy-start.2 = (bf16[4,128,4096]{2,1,0:T(8,128)(2,1)S(1)}, bf16[4,128,4096]{2,1,0:T(8,128)(2,1)}, u32[]{:S(2)}) copy-start(bf16[4,128,4096]{2,1,0:T(8,128)(2,1)} %all-gather.3.cloned.1.call-done) | copy-start | bytes 12582916
  118.8 8.8 %copy-start.6 = (bf16[896,64]{0,1:T(8,128)(2,1)S(1)}, bf16[896,64]{0,1:T(8,128)(2,1)}, u32[]{:S(2)}) copy-start(bf16[896,64]{0,1:T(8,128)(2,1)} %param.22) | copy-start | bytes 344068
  128.8 1.5 copy-start.7
  130.3 1.3 copy-start.4
  186.4 3.1 %copy-start.5 = (bf16[32,6144]{1,0:T(8,128)(2,1)S(1)}, bf16[32,6144]{1,0:T(8,128)(2,1)}, u32[]{:S(2)}) copy-start(bf16[32,6144]{1,0:T(8,128)(2,1)} %param.23) | copy-start | bytes 1179652
Sparse Core Ops, SparseCore 0:
  32.5 36.4 all-gather.4
  70.9 37.3 all-gather.2
  131.7 54.6 all-reduce.2
where the time goes:
time: 219 us; the launch traced here: 218 us
  waiting for transfers between devices  96.7 us (44%)
  blocking collectives  57.1 us (26%)
  matrix products  43 us (20%)
  between operations  13.9 us (6%)
  other arithmetic  5.9 us (3%)
    psum x1, waiting for transfers between devices, body(): lax.psum((a_part, b_up_part, b_gate_part), ('dp', 'pipe'))  51.3 us
    all_gather x1, waiting for transfers between devices, body(): lax.all_gather(sent_in, ('dp', 'pipe'), axis=2, tiled=True)  26.9 us
    all_to_all x1, blocking collectives, body(): lax.all_to_all(buffer_back.reshape(experts, capacity, columns), 'expert',...  20.9 us
    all_gather x1, waiting for transfers between devices, body(): lax.all_gather(sent_back, ('dp', 'pipe'), axis=2, tiled=True)  18.5 us
    all_to_all x1, blocking collectives, body(): lax.all_to_all(buffer_in.reshape(experts, capacity, columns), 'expert', s...  16.8 us
    dot_general x1, matrix products, body(): gate_pre = jnp.dot(slot_in, gate_proj, preferred_element_type=jnp.float32)  10.5 us
    all_to_all x1, blocking collectives, send_back(): lax.all_to_all(scores, 'expert', split_axis=0, concat_axis=0, tiled=True)  10.1 us
    psum x1, blocking collectives, body(): totals = lax.psum(partial_sum, 'expert')  9.28 us
  transfers between devices with their start and end apart: 3, of which 3 were waited for; matrix products, arithmetic and copies ran while one was open for 8% of the time, Pallas kernels for 0%

commit v1 on v0

v1 whole, which is shorter than its diff:
```python
import functools
import math

import jax
import jax.numpy as jnp
from jax import lax
from jax.experimental import pallas as pl
from jax.experimental.pallas import tpu as pltpu
from jax.sharding import PartitionSpec as P


PLANE = ("dp", "pipe")
F32 = jnp.float32
BF16 = jnp.bfloat16
NT = (((1,), (1,)), ((), ()))


def slot_matrix(route_rows, gate_rows, experts, capacity):
    count = route_rows.shape[0]
    flat = route_rows.reshape(-1)
    labels = jnp.arange(experts, dtype=jnp.int32)
    onehot = (flat[:, None] == labels[None, :]).astype(jnp.int32)
    earlier = jnp.cumsum(onehot, axis=0) - onehot
    position = jnp.sum(onehot * (labels[None, :] * capacity + earlier), axis=1)
    slot_ids = jnp.arange(experts * capacity, dtype=jnp.int32)
    table = (
        (position[None, :] == slot_ids[:, None])
        .astype(jnp.float32)
        .reshape(experts * capacity, count, 2)
    )
    picks = jnp.sum(table, axis=2)
    weighted = jnp.sum(table * gate_rows[None, :, :], axis=2)
    return (picks, weighted)


def slot_body(
    inputs,
    cotangents,
    routes,
    gates,
    w_gate,
    w_up,
    w_down,
    proj_in,
    proj_out,
    proj_hid_a,
    proj_hid_b,
    queries,
):
    experts = lax.axis_size("expert")
    count, width = inputs.shape
    capacity = 4 * count // experts
    query_count = queries.shape[0]
    picks, weighted = slot_matrix(routes, gates, experts, capacity)
    pick_rows = picks.astype(BF16)
    columns = width // lax.axis_size(PLANE)
    start = lax.axis_index(PLANE) * columns

    def dispatch(rows):
        part = lax.dynamic_slice_in_dim(rows, start, columns, 1)
        buffer = jnp.dot(pick_rows, part, preferred_element_type=F32).astype(BF16)
        sent = lax.all_to_all(
            buffer.reshape(experts, capacity, columns),
            "expert",
            split_axis=0,
            concat_axis=0,
            tiled=True,
        )
        return lax.all_gather(sent, PLANE, axis=2, tiled=True).reshape(-1, width)

    slot_in, slot_back = dispatch(inputs), dispatch(cotangents)
    gate_pre = jnp.dot(slot_in, w_gate[0], preferred_element_type=F32)
    up_pre = jnp.dot(slot_in, w_up[0], preferred_element_type=F32)
    sigma = jax.nn.sigmoid(gate_pre)
    hidden = (gate_pre * sigma * up_pre).astype(BF16)
    back = lax.dot_general(slot_back, w_down[0], NT, preferred_element_type=F32)
    d_up = (back * gate_pre * sigma).astype(BF16)
    d_gate = (back * up_pre * sigma * (1.0 + gate_pre * (1.0 - sigma))).astype(BF16)
    a_hidden, b_up, b_gate = lax.psum(
        (
            jnp.dot(hidden, proj_hid_a, preferred_element_type=F32),
            jnp.dot(d_up, proj_hid_b, preferred_element_type=F32),
            jnp.dot(d_gate, proj_hid_b, preferred_element_type=F32),
        ),
        PLANE,
    )
    a_input = jnp.dot(slot_in, proj_in, preferred_element_type=F32)
    b_output = jnp.dot(slot_back, proj_out, preferred_element_type=F32)
    height = slot_in.shape[0]
    sketch = jnp.concatenate(
        [
            (a_hidden[:, :, None] * b_output[:, None, :]).reshape(height, -1),
            (a_input[:, :, None] * b_up[:, None, :]).reshape(height, -1),
            (a_input[:, :, None] * b_gate[:, None, :]).reshape(height, -1),
        ],
        axis=1,
    ).astype(BF16)
    scores = lax.dot_general(sketch, queries, NT, preferred_element_type=F32)
    returned = lax.all_to_all(
        scores.reshape(experts, capacity, query_count),
        "expert",
        split_axis=0,
        concat_axis=0,
        tiled=True,
    )
    token_scores = lax.dot_general(
        weighted,
        returned.reshape(-1, query_count),
        (((0,), (0,)), ((), ())),
        precision=lax.Precision.HIGHEST,
        preferred_element_type=F32,
    )
    scale = 1.0 / math.sqrt(count * experts)
    totals = lax.psum(jnp.sum(token_scores, axis=0), "expert")
    return (token_scores, totals * scale)


def hidden_kernel(blocks, order_ref, *refs):
    n = 1 + max(ref for block in blocks for _, _, *pair in block for ref, _ in pair)
    rows, (wg, wu, wd, pha, phb, out) = refs[:n], refs[n : n + 6]
    xs, gs, wgs, wus, wds, acc_g, acc_u, acc_b, hid, dup, dgate, sems, row_sems = refs[n + 6 :]
    steps, tall, cut = xs.shape
    count = tall // len(blocks)
    core = order_ref[steps]
    ka, kb = pha.shape[0], phb.shape[0]

    moves = [[[], []] for _ in range(steps)]
    for s, block in enumerate(blocks):
        for i, part, *pair in block:
            for kind, (ref, at) in enumerate(pair):
                here = (xs, gs)[kind].at[i, pl.ds(s * count, count)]
                if part is None:
                    there = rows[ref].at[:, pl.ds(pl.multiple_of(order_ref[i] * cut, cut), cut)]
                else:
                    there = rows[ref].at[at]
                    lane = (core if part == 0 else 1 - core) * (cut // 2)
                    here = here.at[:, pl.ds(pl.multiple_of(lane, cut // 2), cut // 2)]
                moves[i][kind].append((there, here))
    copies = []
    for i in range(steps):
        at = pl.ds(pl.multiple_of(order_ref[i] * cut, cut), cut)
        lanes = [
            [(wg.at[0, at], wgs.at[i])],
            moves[i][0],
            [(wu.at[0, at], wus.at[i])],
            moves[i][1],
            [(wd.at[0, :, at], wds.at[i])],
        ]
        made = []
        k = 0
        for lane_no, lane in enumerate(lanes):
            group = []
            for src, dst in lane:
                if lane_no in (1, 3):
                    sem = row_sems.at[i, k]
                    k += 1
                else:
                    sem = sems.at[i, lane_no // 2]
                group.append(pltpu.make_async_copy(src, dst, sem))
            made.append(group)
        copies.append(made)
    for made in copies:
        for group in made:
            for copy in group:
                copy.start()

    def put(acc, i, value):
        if i:
            acc[...] += value
        else:
            acc[...] = value

    for i in range(steps):
        gate_w, x_rows, up_w, g_rows, down_w = copies[i]
        for copy in gate_w + x_rows:
            copy.wait()
        put(acc_g, i, jnp.dot(xs[i], wgs[i], preferred_element_type=F32))
        for copy in up_w:
            copy.wait()
        put(acc_u, i, jnp.dot(xs[i], wus[i], preferred_element_type=F32))
        for copy in g_rows + down_w:
            copy.wait()
        put(acc_b, i, lax.dot_general(gs[i], wds[i], NT, preferred_element_type=F32))

    high = 16

    def nonlinear(i, carry):
        at = pl.ds(pl.multiple_of(i * high, high), high)
        gate, up, back = acc_g[at, :], acc_u[at, :], acc_b[at, :]
        sigma = jax.nn.sigmoid(gate)
        act = gate * sigma
        hid[at, :] = (act * up).astype(BF16)
        dup[at, :] = (back * act).astype(BF16)
        dgate[at, :] = (back * up * sigma * (1.0 + gate * (1.0 - sigma))).astype(BF16)
        return carry

    lax.fori_loop(0, tall // high, nonlinear, 0, unroll=2)
    out[:ka] = lax.dot_general(pha[...], hid[...], NT, preferred_element_type=F32)
    out[ka : ka + kb] = lax.dot_general(phb[...], dup[...], NT, preferred_element_type=F32)
    out[ka + kb :] = lax.dot_general(phb[...], dgate[...], NT, preferred_element_type=F32)


def hidden_call(blocks, rows, order, count, weights):
    w_gate, w_up, w_down, pha, phb = weights
    width, units = w_gate.shape[1:]
    steps = order.shape[0] - 1
    cut = width // steps
    ka, kb = pha.shape[0], phb.shape[0]
    tall = count * len(blocks)
    most = 2 * sum(1 for block in blocks for i, *_ in block if i == 0)
    anywhere = pl.BlockSpec(memory_space=pl.ANY)
    return pl.pallas_call(
        functools.partial(hidden_kernel, blocks),
        in_specs=[pl.BlockSpec(memory_space=pltpu.SMEM)]
        + [anywhere] * (len(rows) + 3)
        + [pl.BlockSpec(memory_space=pltpu.VMEM)] * 2,
        out_specs=pl.BlockSpec(memory_space=pltpu.VMEM),
        out_shape=jax.ShapeDtypeStruct((ka + 2 * kb, tall), F32),
        scratch_shapes=[
            pltpu.VMEM((steps, tall, cut), BF16),
            pltpu.VMEM((steps, tall, cut), BF16),
            pltpu.VMEM((steps, cut, units), BF16),
            pltpu.VMEM((steps, cut, units), BF16),
            pltpu.VMEM((steps, units, cut), BF16),
        ]
        + [pltpu.VMEM((tall, units), F32)] * 3
        + [pltpu.VMEM((tall, units), BF16)] * 3
        + [pltpu.SemaphoreType.DMA((steps, 3)), pltpu.SemaphoreType.DMA((steps, most))],
        cost_estimate=pl.CostEstimate(
            flops=6 * tall * width * units, bytes_accessed=6 * width * units, transcendentals=0
        ),
    )(order, *rows, w_gate, w_up, w_down, pha, phb)


def score_kernel(ka, kb, place_ref, keep_ref, other_ref, q_ref, *refs):
    n = len(refs) // 2
    notes, outs = refs[:n], refs[n:]
    core, z = place_ref[0], place_ref[1]
    keep, other = keep_ref[...], other_ref[...]
    part = jnp.concatenate(
        [jnp.where(core == 0, keep, other), jnp.where(core == 0, other, keep)], axis=1
    )
    full = jnp.concatenate([note[: ka + kb] for note in notes], axis=1)
    scale = jnp.concatenate([note[pl.ds(ka + kb + z, 1), :] for note in notes], axis=1)
    a_hid, b_up, b_gate = part[:ka], part[ka : ka + kb], part[ka + kb :]
    a_in, b_out = full[:ka], full[ka:]
    nq = q_ref.shape[0]
    total = None
    group = 256 // kb
    base = 0
    for a, b in ((a_hid, b_out), (a_in, b_up), (a_in, b_gate)):
        for i in range(0, ka, group):
            block = jnp.concatenate(
                [(a[i + j : i + j + 1] * b).astype(BF16) for j in range(group)], axis=0
            )
            term = jnp.dot(q_ref[:, base : base + group * kb], block, preferred_element_type=F32)
            total = term if total is None else total + term
            base += group * kb
    total = total * scale
    ones = jnp.ones((8, total.shape[1]), F32)
    sums = lax.dot_general(
        ones, total, NT, precision=lax.Precision.HIGHEST, preferred_element_type=F32
    )
    count = outs[0].shape[1]
    sums = jnp.concatenate([sums, jnp.zeros((8, count - nq), F32)], axis=1)
    for s, out in enumerate(outs):
        out[:nq] = total[:, s * count : (s + 1) * count]
        out[nq:] = sums


def last_kernel(scale, place_ref, *refs):
    pieces, (tokens, totals) = refs[:-2], refs[-2:]
    z = place_ref[1]
    n = len(pieces)
    nq = tokens.shape[0]
    tokens[...] = functools.reduce(jnp.add, [p[:nq] for p in pieces])
    sums = [p[nq : nq + 1] for p in pieces]
    total = None
    for e in range(n):
        term = sums[0]
        for s in range(1, n):
            term = jnp.where(lax.rem(z + s, n) == e, sums[s], term)
        total = term if total is None else total + term
    totals[...] = total * scale


def token_body(
    inputs,
    cotangents,
    routes,
    gates,
    w_gate,
    w_up,
    w_down,
    proj_in,
    proj_out,
    proj_hid_a,
    proj_hid_b,
    queries,
):
    experts = lax.axis_size("expert")
    cores = 2
    ys, xs = lax.axis_size("dp") // cores, lax.axis_size("pipe")
    chips = ys * xs
    count, width = inputs.shape
    nq = queries.shape[0]
    ka, kb = proj_hid_a.shape[1], proj_hid_b.shape[1]
    dp, x, z = lax.axis_index("dp"), lax.axis_index("pipe"), lax.axis_index("expert")
    y, core = dp // cores, dp % cores
    cut = width // (chips * cores)

    def over_z(value, shift):
        pairs = [(i, (i + shift) % experts) for i in range(experts)]
        return lax.ppermute(value, "expert", pairs)

    def over_plane(value, dy, dc, dx):
        pairs = []
        for i in range(ys):
            for c in range(cores):
                for k in range(xs):
                    to = (((i + dy) % ys) * cores + (c + dc) % cores) * xs + (k + dx) % xs
                    pairs.append(((i * cores + c) * xs + k, to))
        return lax.ppermute(value, PLANE, pairs)

    def swap(value):
        return over_plane(value, 0, 1, 0)

    offsets = [(dy, dx) for dy in range(ys) for dx in range(xs)]
    chip_at = [((y - dy) % ys) * xs + (x - dx) % xs for dy, dx in offsets]
    order = jnp.stack([*chip_at, core]).astype(jnp.int32)
    place = jnp.stack([core, z]).astype(jnp.int32)
    weights = (w_gate, w_up, w_down, proj_hid_a.T, proj_hid_b.T)

    def piece_of(chip):
        start = (chip * cores + core) * cut
        return jnp.stack(
            [
                lax.dynamic_slice_in_dim(inputs, start, cut, 1),
                lax.dynamic_slice_in_dim(cotangents, start, cut, 1),
            ]
        )

    shifts = list(range(1, experts))
    piece = piece_of(chip_at[0])
    across = len(offsets) - 1 if ys > 1 and xs > 1 else 0
    extra = piece_of(chip_at[across]) if across else None
    came = {}
    for s in shifts:
        came[s] = over_z(piece, s)
    came_extra = over_z(extra, shifts[-1]) if across else None

    labels = jnp.arange(experts, dtype=jnp.int32)
    named = (routes.T[:, None, :] == labels[None, :, None]).astype(F32)
    table = jnp.sum(named * gates.T[:, None, :], axis=0)
    down = (((0,), (1,)), ((), ()))
    note = jnp.concatenate(
        [
            lax.dot_general(proj_in, inputs, down, preferred_element_type=F32),
            lax.dot_general(proj_out, cotangents, down, preferred_element_type=F32),
            table,
        ],
        axis=0,
    )
    notes = [note]
    for s in shifts:
        notes.append(over_z(note, s))

    def spread(s):
        found = []
        for i, (dy, dx) in enumerate(offsets):
            if i == 0:
                near = came[s]
            elif s == shifts[-1] and i == across:
                near = came_extra
            else:
                near = over_plane(came[s], dy, 0, dx)
            found.append((i, near))
        return found

    def block_rows(spreads):
        rows, blocks = [], []
        for near_pieces in spreads:
            block = []
            for i, near in near_pieces:
                for part, array in enumerate((near, swap(near))):
                    block.append((i, part, (len(rows), 0), (len(rows), 1)))
                    rows.append(array)
            blocks.append(block)
        return rows, blocks

    near = {s: spread(s) for s in shifts}
    early = shifts[: experts // 2 - 1]
    late = shifts[experts // 2 - 1 :]
    rows, blocks = block_rows([near[s] for s in early])
    base = len(rows)
    own = [(i, None, (base, 0), (base + 1, 0)) for i in range(chips)]
    first = hidden_call(
        [own] + blocks, [*rows, inputs, cotangents], order, count, weights
    )
    rows, blocks = block_rows([near[s] for s in late])
    second = hidden_call(blocks, rows, order, count, weights)

    keep = jnp.where(core == 0, first, second) + swap(jnp.where(core == 0, second, first))
    sent = keep.astype(BF16)
    for dy, dx in offsets[1:]:
        keep = keep + over_plane(sent, dy, 0, dx).astype(F32)
    other = swap(keep)

    smem = pl.BlockSpec(memory_space=pltpu.SMEM)
    vmem = pl.BlockSpec(memory_space=pltpu.VMEM)
    scored = pl.pallas_call(
        functools.partial(score_kernel, ka, kb),
        in_specs=[smem] + [vmem] * (3 + experts),
        out_specs=[vmem] * experts,
        out_shape=[jax.ShapeDtypeStruct((nq + 8, count), F32)] * experts,
    )(place, keep, other, queries, *notes)
    back = [scored[0]] + [over_z(scored[s], -s) for s in shifts]
    tokens, totals = pl.pallas_call(
        functools.partial(last_kernel, 1.0 / math.sqrt(count * experts)),
        in_specs=[smem] + [vmem] * experts,
        out_specs=[vmem] * 2,
        out_shape=[
            jax.ShapeDtypeStruct((nq, count), F32),
            jax.ShapeDtypeStruct((1, count), F32),
        ],
    )(place, *back)
    return (tokens.T, totals[0, :nq])


def solution(mesh):
    placed = (
        P("expert", None),
        P("expert", None),
        P("expert", None),
        P("expert", None),
        P("expert", None, PLANE),
        P("expert", None, PLANE),
        P("expert", PLANE, None),
        P(),
        P(),
        P(PLANE, None),
        P(PLANE, None),
        P(PLANE, None),
    )

    experts, dp, _ = (mesh.shape[name] for name in ("expert", "dp", "pipe"))
    whole = experts <= 4 and experts % 2 + dp % 2 == 0

    def body(*args):
        if not whole:
            return slot_body(*args)
        return token_body(*args)

    return jax.shard_map(
        body,
        mesh=mesh,
        in_specs=placed,
        out_specs=(P("expert", PLANE), P(PLANE)),
        check_vma=False,
    )
```

time: 219 us -> 126 us (0.58)
  blocking collectives: 57.1 us -> 0 us
  waiting for transfers between devices: 96.7 us -> 40 us
  starting transfers between devices: 0.12 us -> 41.9 us
  matrix products: 43 us -> 2.15 us
  Pallas kernels: 0 us -> 33.5 us
  between operations: 13.9 us -> 1.08 us
  other arithmetic: 5.9 us -> 1.69 us
  local copies, waits for them, and re-layouts: 1.66 us -> 5.23 us
    psum x1 -> x0, waiting for transfers between devices: 51.3 us -> none  [body(): lax.psum((a_part, b_up_part, b_gate_part), ('dp', 'pipe'))]
    all_to_all x3 -> x0, blocking collectives: 47.8 us -> none  [the longest x1 20.9 us: body(): lax.all_to_all(buffer_back.reshape(experts, capacity, columns), 'expert',...]
    all_gather x2 -> x0, waiting for transfers between devices: 45.4 us -> none  [the longest x1 26.9 us: body(): lax.all_gather(sent_in, ('dp', 'pipe'), axis=2, tiled=True)]
    ppermute x0 -> x35, starting transfers between devices: none -> 41.9 us  [the longest x10 23.3 us: over_z(): return lax.ppermute(value, 'expert', pairs)]
    dot_general x12 -> x2, matrix products: 43 us -> 2.15 us  [the longest x1 1.7 us: token_body(): lax.dot_general(proj_out, cotangents, down, preferred_element_type=F32)]
    ppermute x0 -> x35, waiting for transfers between devices: none -> 40 us  [the longest x10 21.5 us: over_z(): return lax.ppermute(value, 'expert', pairs)]
    pallas_call x0 -> x4, Pallas kernels: none -> 33.5 us  [the longest x2 28.9 us: hidden_call(): pl.pallas_call(functools.partial(hidden_kernel, blocks), in_specs=[pl.Blo...]
    psum x1 -> x0, blocking collectives: 9.28 us -> none  [body(): totals = lax.psum(partial_sum, 'expert')]
  transfers between devices with their start and end apart: 3 -> 35, of which waited for: 3 -> 15; matrix products, arithmetic and copies ran while one was open for 8% -> 3% of each run, Pallas kernels for 0% -> 11%
where the time goes in v1:
time: 126 us
  starting transfers between devices  41.9 us (33%)
  waiting for transfers between devices  40 us (32%)
  Pallas kernels  33.5 us (27%)
  local copies, waits for them, and re-layouts  5.23 us (4%)
  matrix products  2.15 us (2%)
  other arithmetic  1.69 us (1%)
    pallas_call x2, Pallas kernels, hidden_call(): pl.pallas_call(functools.partial(hidden_kernel, blocks), in_specs=[pl.Blo...  28.9 us
    ppermute x10, starting transfers between devices, over_z(): return lax.ppermute(value, 'expert', pairs)  23.3 us
    ppermute x10, waiting for transfers between devices, over_z(): return lax.ppermute(value, 'expert', pairs)  21.5 us
    ppermute x25, starting transfers between devices, over_plane(): return lax.ppermute(value, PLANE, pairs)  18.6 us
    ppermute x25, waiting for transfers between devices, over_plane(): return lax.ppermute(value, PLANE, pairs)  18.6 us
    pallas_call x1, Pallas kernels, token_body(): pl.pallas_call(functools.partial(score_kernel, ka, kb), in_specs=[smem] +...  3.23 us
  transfers between devices with their start and end apart: 35, of which 15 were waited for; matrix products, arithmetic and copies ran while one was open for 3% of the time, Pallas kernels for 11%

profile of v1, /device:TPU:0, one launch (start us, length us, event | category | flops | bytes accessed | tf_op | source)
XLA Modules:
  0.0 125.6 jit_solution(8936720165181636125)
XLA Ops:
  0.7 1.2 dynamic-slice_bitcast_fusion
  2.0 3.1 %collective-permute-start = (bf16[2,128,512]{2,1,0:T(8,128)(2,1)S(1)}, bf16[2,128,512]{2,1,0:T(8,128)(2,1)S(1)}, u32[]{:S(2)}, u32[]{:S(2)}) collective-permute-start(bf16[2,128,512]{2,1,0:T(8,128)(2,1)S(1)} %pad_maximum_fusion), channel_id=1, source_target_pairs={{0,2},{2,4},{4,6},{6,0},{1,3},{3,5},{5,7},{7,1},{8,10},{10,12},{12... | collective-permute-start | bytes 786440 | tf_op jit(solution)/shard_map/ppermute | solution.py:314
  5.1 2.1 %collective-permute-start.22 = (bf16[2,128,512]{2,1,0:T(8,128)(2,1)S(1)}, bf16[2,128,512]{2,1,0:T(8,128)(2,1)S(1)}, u32[]{:S(2)}, u32[]{:S(2)}) collective-permute-start(bf16[2,128,512]{2,1,0:T(8,128)(2,1)S(1)} %pad_maximum_fusion.1), channel_id=1, source_target_pairs={{0,6},{2,0},{4,2},{6,4},{1,7},{3,1},{5,3},{7,5},{8,14},{10,8},{12,... | collective-permute-start | bytes 786440 | tf_op jit(solution)/shard_map/ppermute | solution.py:314
  8.2 1.3 %collective-permute-start.16 = (bf16[2,128,512]{2,1,0:T(8,128)(2,1)S(1)}, bf16[2,128,512]{2,1,0:T(8,128)(2,1)S(1)}, u32[]{:S(2)}, u32[]{:S(2)}) collective-permute-start(bf16[2,128,512]{2,1,0:T(8,128)(2,1)S(1)} %pad_maximum_fusion), channel_id=1, source_target_pairs={{0,6},{2,0},{4,2},{6,4},{1,7},{3,1},{5,3},{7,5},{8,14},{10,8},{12,... | collective-permute-start | bytes 786440 | tf_op jit(solution)/shard_map/ppermute | solution.py:314
  9.5 4.8 %collective-permute-done.refs_0_ = bf16[2,128,512]{2,1,0:T(8,128)(2,1)S(1)} collective-permute-done((bf16[2,128,512]{2,1,0:T(8,128)(2,1)S(1)}, bf16[2,128,512]{2,1,0:T(8,128)(2,1)S(1)}, u32[]{:S(2)}, u32[]{:S(2)}) %collective-permute-start) | collective-permute-done | bytes 262176 | tf_op jit(solution)/shard_map/ppermute | solution.py:314
  14.3 1.7 %collective-permute-start.2 = (bf16[2,128,512]{2,1,0:T(8,128)(2,1)S(1)}, bf16[2,128,512]{2,1,0:T(8,128)(2,1)S(1)}, u32[]{:S(2)}, u32[]{:S(2)}) collective-permute-start(bf16[2,128,512]{2,1,0:T(8,128)(2,1)S(1)} %collective-permute-done.refs_0_), channel_id=1, source_target_pairs={{0,1},{1,0},{8,9},{9,8},{16,17},{17,16},{24,25},{25,24},{2,3},{3,2... | collective-permute-start | bytes 786440 | tf_op jit(solution)/shard_map/ppermute | solution.py:323
  16.0 1.5 %collective-permute-start.4 = (bf16[2,128,512]{2,1,0:T(8,128)(2,1)S(1)}, bf16[2,128,512]{2,1,0:T(8,128)(2,1)S(1)}, u32[]{:S(2)}, u32[]{:S(2)}) collective-permute-start(bf16[2,128,512]{2,1,0:T(8,128)(2,1)S(1)} %collective-permute-done.refs_0_), channel_id=1, source_target_pairs={{0,16},{1,17},{8,24},{9,25},{16,0},{17,1},{24,8},{25,9},{2,18},{3,... | collective-permute-start | bytes 786440 | tf_op jit(solution)/shard_map/ppermute | solution.py:323
  17.5 1.6 %collective-permute-done.22.refs_14_ = bf16[2,128,512]{2,1,0:T(8,128)(2,1)S(1)} collective-permute-done((bf16[2,128,512]{2,1,0:T(8,128)(2,1)S(1)}, bf16[2,128,512]{2,1,0:T(8,128)(2,1)S(1)}, u32[]{:S(2)}, u32[]{:S(2)}) %collective-permute-start.22) | collective-permute-done | bytes 262176 | tf_op jit(solution)/shard_map/ppermute | solution.py:314
  19.1 2.4 %collective-permute-start.6 = (bf16[2,128,512]{2,1,0:T(8,128)(2,1)S(1)}, bf16[2,128,512]{2,1,0:T(8,128)(2,1)S(1)}, u32[]{:S(2)}, u32[]{:S(2)}) collective-permute-start(bf16[2,128,512]{2,1,0:T(8,128)(2,1)S(1)} %collective-permute-done.refs_0_), channel_id=1, source_target_pairs={{0,17},{1,16},{8,25},{9,24},{16,1},{17,0},{24,9},{25,8},{2,19},{3,... | collective-permute-start | bytes 786440 | tf_op jit(solution)/shard_map/ppermute | solution.py:323
  21.6 8.8 %collective-permute-done.8.refs_0_ = bf16[2,128,512]{2,1,0:T(8,128)(2,1)S(1)} collective-permute-done((bf16[2,128,512]{2,1,0:T(8,128)(2,1)S(1)}, bf16[2,128,512]{2,1,0:T(8,128)(2,1)S(1)}, u32[]{:S(2)}, u32[]{:S(2)}) %collective-permute-start.8) | collective-permute-done | bytes 262176 | tf_op jit(solution)/shard_map/ppermute | solution.py:314
  30.9 1.5 %collective-permute-start.10 = (bf16[2,128,512]{2,1,0:T(8,128)(2,1)S(1)}, bf16[2,128,512]{2,1,0:T(8,128)(2,1)S(1)}, u32[]{:S(2)}, u32[]{:S(2)}) collective-permute-start(bf16[2,128,512]{2,1,0:T(8,128)(2,1)S(1)} %collective-permute-done.8.refs_0_), channel_id=1, source_target_pairs={{0,1},{1,0},{8,9},{9,8},{16,17},{17,16},{24,25},{25,24},{2,3},{3,2... | collective-permute-start | bytes 786440 | tf_op jit(solution)/shard_map/ppermute | solution.py:323
  32.4 1.5 %collective-permute-start.12 = (bf16[2,128,512]{2,1,0:T(8,128)(2,1)S(1)}, bf16[2,128,512]{2,1,0:T(8,128)(2,1)S(1)}, u32[]{:S(2)}, u32[]{:S(2)}) collective-permute-start(bf16[2,128,512]{2,1,0:T(8,128)(2,1)S(1)} %collective-permute-done.8.refs_0_), channel_id=1, source_target_pairs={{0,16},{1,17},{8,24},{9,25},{16,0},{17,1},{24,8},{25,9},{2,18},{3,... | collective-permute-start | bytes 786440 | tf_op jit(solution)/shard_map/ppermute | solution.py:323
  34.4 1.5 %collective-permute-start.18 = (bf16[2,128,512]{2,1,0:T(8,128)(2,1)S(1)}, bf16[2,128,512]{2,1,0:T(8,128)(2,1)}, u32[]{:S(2)}, u32[]{:S(2)}) collective-permute-start(bf16[2,128,512]{2,1,0:T(8,128)(2,1)S(1)} %collective-permute-done.16.refs_8_), channel_id=1, source_target_pairs={{0,1},{1,0},{8,9},{9,8},{16,17},{17,16},{24,25},{25,24},{2,3},{3,2... | collective-permute-start | bytes 786440 | tf_op jit(solution)/shard_map/ppermute | solution.py:323
  35.9 1.6 %collective-permute-start.20 = (bf16[2,128,512]{2,1,0:T(8,128)(2,1)S(1)}, bf16[2,128,512]{2,1,0:T(8,128)(2,1)}, u32[]{:S(2)}, u32[]{:S(2)}) collective-permute-start(bf16[2,128,512]{2,1,0:T(8,128)(2,1)S(1)} %collective-permute-done.16.refs_8_), channel_id=1, source_target_pairs={{0,16},{1,17},{8,24},{9,25},{16,0},{17,1},{24,8},{25,9},{2,18},{3,... | collective-permute-start | bytes 786440 | tf_op jit(solution)/shard_map/ppermute | solution.py:323
  38.1 1.9 %collective-permute-done.10.refs_2_ = bf16[2,128,512]{2,1,0:T(8,128)(2,1)S(1)} collective-permute-done((bf16[2,128,512]{2,1,0:T(8,128)(2,1)S(1)}, bf16[2,128,512]{2,1,0:T(8,128)(2,1)S(1)}, u32[]{:S(2)}, u32[]{:S(2)}) %collective-permute-start.10) | collective-permute-done | bytes 262176 | tf_op jit(solution)/shard_map/ppermute | solution.py:323
  40.1 7.1 %collective-permute-done.12.refs_4_ = bf16[2,128,512]{2,1,0:T(8,128)(2,1)S(1)} collective-permute-done((bf16[2,128,512]{2,1,0:T(8,128)(2,1)S(1)}, bf16[2,128,512]{2,1,0:T(8,128)(2,1)S(1)}, u32[]{:S(2)}, u32[]{:S(2)}) %collective-permute-start.12) | collective-permute-done | bytes 262176 | tf_op jit(solution)/shard_map/ppermute | solution.py:323
  47.7 2.9 %collective-permute-done.18.refs_10_ = bf16[2,128,512]{2,1,0:T(8,128)(2,1)} collective-permute-done((bf16[2,128,512]{2,1,0:T(8,128)(2,1)S(1)}, bf16[2,128,512]{2,1,0:T(8,128)(2,1)}, u32[]{:S(2)}, u32[]{:S(2)}) %collective-permute-start.18) | collective-permute-done | bytes 262176 | tf_op jit(solution)/shard_map/ppermute | solution.py:323
  51.7 1.7 %fusion.2 = f32[64,128]{1,0:T(8,128)S(1)} fusion(bf16[4096,64]{0,1:T(8,128)(2,1)S(1)} %copy-done, bf16[128,4096]{1,0:T(8,128)(2,1)} %refs_9_.1), kind=kOutput, calls=%fused_computation.16 | convolution fusion | flops 67108864 | bytes 1605632 | tf_op jit(solution)/shard_map/dot_general | solution.py:359
  55.4 14.3 %shard_map.131 = f32[160,256]{1,0:T(8,128)} custom-call(s32[5]{0:T(128)} %stack.50.order_ref, bf16[2,128,512]{2,1,0:T(8,128)(2,1)} %copy-done.7, bf16[2,128,512]{2,1,0:T(8,128)(2,1)} %copy-done.14, bf16[2,128,512]{2,1,0:T(8,128)(2,1)} %copy-done.8, bf16[2,128,512]{2,1,0:T(8,128)(2,1)} %copy-done.17, bf16[2,128,512]{2,1,0:T(8,128)(2,1)} %copy-done.10, ...), custom_call_target="tpu_custom_call" | custom-call | flops 5637144576 | bytes 22020096 | tf_op jit(solution)/shard_map/pallas_call | solution.py:212
  69.9 14.5 %shard_map.132 = f32[160,256]{1,0:T(8,128)} custom-call(s32[5]{0:T(128)} %stack.50.order_ref, bf16[2,128,512]{2,1,0:T(8,128)(2,1)} %copy-done.5, bf16[2,128,512]{2,1,0:T(8,128)(2,1)} %copy-done.16, bf16[2,128,512]{2,1,0:T(8,128)(2,1)} %copy-done.11, bf16[2,128,512]{2,1,0:T(8,128)(2,1)} %collective-permute-done.11.refs_3_, bf16[2,128,512]{2,1,0:T(8,128)(2,1)} %copy-done.13, ...), custom_call_target="tpu_custom_call" | custom-call | flops 5637144576 | bytes 22020096 | tf_op jit(solution)/shard_map/pallas_call | solution.py:212
  87.7 1.5 %collective-permute-start.26 = (bf16[160,256]{1,0:T(8,128)(2,1)S(1)}, bf16[160,256]{1,0:T(8,128)(2,1)S(1)}, u32[]{:S(2)}, u32[]{:S(2)}) collective-permute-start(bf16[160,256]{1,0:T(8,128)(2,1)S(1)} %get-tuple-element.14), channel_id=1, source_target_pairs={{0,16},{1,17},{8,24},{9,25},{16,0},{17,1},{24,8},{25,9},{2,18},{3,... | collective-permute-start | bytes 245768 | tf_op jit(solution)/shard_map/ppermute | solution.py:323
  89.2 1.2 collective-permute-start.27
  90.5 1.7 %collective-permute-done.25 = bf16[160,256]{1,0:T(8,128)(2,1)S(1)} collective-permute-done((bf16[160,256]{1,0:T(8,128)(2,1)S(1)}, bf16[160,256]{1,0:T(8,128)(2,1)S(1)}, u32[]{:S(2)}, u32[]{:S(2)}) %collective-permute-start.25) | collective-permute-done | bytes 81952 | tf_op jit(solution)/shard_map/ppermute | solution.py:323
  92.2 1.5 %collective-permute-done.26 = bf16[160,256]{1,0:T(8,128)(2,1)S(1)} collective-permute-done((bf16[160,256]{1,0:T(8,128)(2,1)S(1)}, bf16[160,256]{1,0:T(8,128)(2,1)S(1)}, u32[]{:S(2)}, u32[]{:S(2)}) %collective-permute-start.26) | collective-permute-done | bytes 81952 | tf_op jit(solution)/shard_map/ppermute | solution.py:323
  93.6 1.3 %collective-permute-done.27 = bf16[160,256]{1,0:T(8,128)(2,1)S(1)} collective-permute-done((bf16[160,256]{1,0:T(8,128)(2,1)S(1)}, bf16[160,256]{1,0:T(8,128)(2,1)S(1)}, u32[]{:S(2)}, u32[]{:S(2)}) %collective-permute-start.27) | collective-permute-done | bytes 81952 | tf_op jit(solution)/shard_map/ppermute | solution.py:323
  95.2 6.2 %collective-permute-start.29 = (f32[100,128]{1,0:T(8,128)S(1)}, f32[100,128]{1,0:T(8,128)S(1)}, u32[]{:S(2)}, u32[]{:S(2)}) collective-permute-start(f32[100,128]{1,0:T(8,128)S(1)} %pad_maximum_fusion.2.refs_0_), channel_id=1, source_target_pairs={{0,2},{2,4},{4,6},{6,0},{1,3},{3,5},{5,7},{7,1},{8,10},{10,12},{12... | collective-permute-start | bytes 153608 | tf_op jit(solution)/shard_map/ppermute | solution.py:314
  101.3 2.0 %collective-permute-start.30 = (f32[100,128]{1,0:T(8,128)S(1)}, f32[100,128]{1,0:T(8,128)S(1)}, u32[]{:S(2)}, u32[]{:S(2)}) collective-permute-start(f32[100,128]{1,0:T(8,128)S(1)} %pad_maximum_fusion.2.refs_0_), channel_id=1, source_target_pairs={{0,4},{2,6},{4,0},{6,2},{1,5},{3,7},{5,1},{7,3},{8,12},{10,14},{12... | collective-permute-start | bytes 153608 | tf_op jit(solution)/shard_map/ppermute | solution.py:314
  103.3 2.8 %collective-permute-start.31 = (f32[100,128]{1,0:T(8,128)S(1)}, f32[100,128]{1,0:T(8,128)S(1)}, u32[]{:S(2)}, u32[]{:S(2)}) collective-permute-start(f32[100,128]{1,0:T(8,128)S(1)} %pad_maximum_fusion.2.refs_0_), channel_id=1, source_target_pairs={{0,6},{2,0},{4,2},{6,4},{1,7},{3,1},{5,3},{7,5},{8,14},{10,8},{12,... | collective-permute-start | bytes 153608 | tf_op jit(solution)/shard_map/ppermute | solution.py:314
  109.2 3.2 %shard_map.133 = (f32[40,128]{1,0:T(8,128)}, f32[40,128]{1,0:T(8,128)}, f32[40,128]{1,0:T(8,128)}, f32[40,128]{1,0:T(8,128)}) custom-call(s32[2]{0:T(128)} %pad_add_fusion.place_ref, f32[160,256]{1,0:T(8,128)} %copy-done.3, f32[160,256]{1,0:T(8,128)} %copy-done.22, bf16[32,6144]{1,0:T(8,128)(2,1)} %q_ref.1, f32[100,128]{1,0:T(8,128)} %copy-done.21, ...), custom_call_target="tpu_custom_call" | custom-call | tf_op jit(solution)/shard_map/pallas_call | solution.py:411
  112.4 4.1 %collective-permute-start.32 = (f32[40,128]{1,0:T(8,128)}, f32[40,128]{1,0:T(8,128)S(1)}, u32[]{:S(2)}, u32[]{:S(2)}) collective-permute-start(f32[40,128]{1,0:T(8,128)} %get-tuple-element.9), channel_id=1, source_target_pairs={{0,6},{2,0},{4,2},{6,4},{1,7},{3,1},{5,3},{7,5},{8,14},{10,8},{12,... | collective-permute-start | bytes 61448 | tf_op jit(solution)/shard_map/ppermute | solution.py:314
  118.3 3.2 %collective-permute-done.33.refs_2_ = f32[40,128]{1,0:T(8,128)S(1)} collective-permute-done((f32[40,128]{1,0:T(8,128)}, f32[40,128]{1,0:T(8,128)S(1)}, u32[]{:S(2)}, u32[]{:S(2)}) %collective-permute-start.33) | collective-permute-done | bytes 20512 | tf_op jit(solution)/shard_map/ppermute | solution.py:314
  123.0 1.4 %shard_map.134 = (f32[32,128]{1,0:T(8,128)}, f32[1,128]{1,0:T(1,128)}) custom-call(s32[2]{0:T(128)} %pad_add_fusion.place_ref, f32[40,128]{1,0:T(8,128)} %get-tuple-element.8.refs_0_, f32[40,128]{1,0:T(8,128)} %copy-done.26, f32[40,128]{1,0:T(8,128)} %copy-done.27, f32[40,128]{1,0:T(8,128)} %copy-done.28), custom_call_target="tpu_custom_call" | custom-call | tf_op jit(solution)/shard_map/pallas_call | solution.py:418
  (117 shorter events, 17.2 us)
Async XLA Ops:
  2.0 12.3 %collective-permute-start = (bf16[2,128,512]{2,1,0:T(8,128)(2,1)S(1)}, bf16[2,128,512]{2,1,0:T(8,128)(2,1)S(1)}, u32[]{:S(2)}, u32[]{:S(2)}) collective-permute-start(bf16[2,128,512]{2,1,0:T(8,128)(2,1)S(1)} %pad_maximum_fusion), channel_id=1, source_target_pairs={{0,2},{2,4},{4,6},{6,0},{1,3},{3,5},{5,7},{7,1},{8,10},{10,12},{12... | collective-permute-start | bytes 786440 | tf_op jit(solution)/shard_map/ppermute | solution.py:314
  5.1 14.0 %collective-permute-start.22 = (bf16[2,128,512]{2,1,0:T(8,128)(2,1)S(1)}, bf16[2,128,512]{2,1,0:T(8,128)(2,1)S(1)}, u32[]{:S(2)}, u32[]{:S(2)}) collective-permute-start(bf16[2,128,512]{2,1,0:T(8,128)(2,1)S(1)} %pad_maximum_fusion.1), channel_id=1, source_target_pairs={{0,6},{2,0},{4,2},{6,4},{1,7},{3,1},{5,3},{7,5},{8,14},{10,8},{12,... | collective-permute-start | bytes 786440 | tf_op jit(solution)/shard_map/ppermute | solution.py:314
  7.2 23.1 %collective-permute-start.8 = (bf16[2,128,512]{2,1,0:T(8,128)(2,1)S(1)}, bf16[2,128,512]{2,1,0:T(8,128)(2,1)S(1)}, u32[]{:S(2)}, u32[]{:S(2)}) collective-permute-start(bf16[2,128,512]{2,1,0:T(8,128)(2,1)S(1)} %pad_maximum_fusion), channel_id=1, source_target_pairs={{0,4},{2,6},{4,0},{6,2},{1,5},{3,7},{5,1},{7,3},{8,12},{10,14},{12... | collective-permute-start | bytes 786440 | tf_op jit(solution)/shard_map/ppermute | solution.py:314
  8.2 22.2 %collective-permute-start.16 = (bf16[2,128,512]{2,1,0:T(8,128)(2,1)S(1)}, bf16[2,128,512]{2,1,0:T(8,128)(2,1)S(1)}, u32[]{:S(2)}, u32[]{:S(2)}) collective-permute-start(bf16[2,128,512]{2,1,0:T(8,128)(2,1)S(1)} %pad_maximum_fusion), channel_id=1, source_target_pairs={{0,6},{2,0},{4,2},{6,4},{1,7},{3,1},{5,3},{7,5},{8,14},{10,8},{12,... | collective-permute-start | bytes 786440 | tf_op jit(solution)/shard_map/ppermute | solution.py:314
  14.3 16.6 %collective-permute-start.2 = (bf16[2,128,512]{2,1,0:T(8,128)(2,1)S(1)}, bf16[2,128,512]{2,1,0:T(8,128)(2,1)S(1)}, u32[]{:S(2)}, u32[]{:S(2)}) collective-permute-start(bf16[2,128,512]{2,1,0:T(8,128)(2,1)S(1)} %collective-permute-done.refs_0_), channel_id=1, source_target_pairs={{0,1},{1,0},{8,9},{9,8},{16,17},{17,16},{24,25},{25,24},{2,3},{3,2... | collective-permute-start | bytes 786440 | tf_op jit(solution)/shard_map/ppermute | solution.py:323
  16.0 16.4 %collective-permute-start.4 = (bf16[2,128,512]{2,1,0:T(8,128)(2,1)S(1)}, bf16[2,128,512]{2,1,0:T(8,128)(2,1)S(1)}, u32[]{:S(2)}, u32[]{:S(2)}) collective-permute-start(bf16[2,128,512]{2,1,0:T(8,128)(2,1)S(1)} %collective-permute-done.refs_0_), channel_id=1, source_target_pairs={{0,16},{1,17},{8,24},{9,25},{16,0},{17,1},{24,8},{25,9},{2,18},{3,... | collective-permute-start | bytes 786440 | tf_op jit(solution)/shard_map/ppermute | solution.py:323
  19.1 14.8 %collective-permute-start.6 = (bf16[2,128,512]{2,1,0:T(8,128)(2,1)S(1)}, bf16[2,128,512]{2,1,0:T(8,128)(2,1)S(1)}, u32[]{:S(2)}, u32[]{:S(2)}) collective-permute-start(bf16[2,128,512]{2,1,0:T(8,128)(2,1)S(1)} %collective-permute-done.refs_0_), channel_id=1, source_target_pairs={{0,17},{1,16},{8,25},{9,24},{16,1},{17,0},{24,9},{25,8},{2,19},{3,... | collective-permute-start | bytes 786440 | tf_op jit(solution)/shard_map/ppermute | solution.py:323
  30.3 4.0 %collective-permute-start.1 = (bf16[2,128,512]{2,1,0:T(8,128)(2,1)S(1)}, bf16[2,128,512]{2,1,0:T(8,128)(2,1)S(1)}, u32[]{:S(2)}, u32[]{:S(2)}) collective-permute-start(bf16[2,128,512]{2,1,0:T(8,128)(2,1)S(1)} %collective-permute-done.refs_0_), channel_id=1, source_target_pairs={{0,8},{1,9},{8,0},{9,1},{16,24},{17,25},{24,16},{25,17},{2,10},{3,... | collective-permute-start | bytes 786440 | tf_op jit(solution)/shard_map/ppermute | solution.py:323
  30.4 5.5 %collective-permute-start.23 = (bf16[2,128,512]{2,1,0:T(8,128)(2,1)S(1)}, bf16[2,128,512]{2,1,0:T(8,128)(2,1)S(1)}, u32[]{:S(2)}, u32[]{:S(2)}) collective-permute-start(bf16[2,128,512]{2,1,0:T(8,128)(2,1)S(1)} %collective-permute-done.22.refs_14_), channel_id=1, source_target_pairs={{0,8},{1,9},{8,0},{9,1},{16,24},{17,25},{24,16},{25,17},{2,10},{3,... | collective-permute-start | bytes 786440 | tf_op jit(solution)/shard_map/ppermute | solution.py:323
  30.9 9.2 %collective-permute-start.10 = (bf16[2,128,512]{2,1,0:T(8,128)(2,1)S(1)}, bf16[2,128,512]{2,1,0:T(8,128)(2,1)S(1)}, u32[]{:S(2)}, u32[]{:S(2)}) collective-permute-start(bf16[2,128,512]{2,1,0:T(8,128)(2,1)S(1)} %collective-permute-done.8.refs_0_), channel_id=1, source_target_pairs={{0,1},{1,0},{8,9},{9,8},{16,17},{17,16},{24,25},{25,24},{2,3},{3,2... | collective-permute-start | bytes 786440 | tf_op jit(solution)/shard_map/ppermute | solution.py:323
  32.4 14.8 %collective-permute-start.12 = (bf16[2,128,512]{2,1,0:T(8,128)(2,1)S(1)}, bf16[2,128,512]{2,1,0:T(8,128)(2,1)S(1)}, u32[]{:S(2)}, u32[]{:S(2)}) collective-permute-start(bf16[2,128,512]{2,1,0:T(8,128)(2,1)S(1)} %collective-permute-done.8.refs_0_), channel_id=1, source_target_pairs={{0,16},{1,17},{8,24},{9,25},{16,0},{17,1},{24,8},{25,9},{2,18},{3,... | collective-permute-start | bytes 786440 | tf_op jit(solution)/shard_map/ppermute | solution.py:323
  33.9 13.3 %collective-permute-start.14 = (bf16[2,128,512]{2,1,0:T(8,128)(2,1)S(1)}, bf16[2,128,512]{2,1,0:T(8,128)(2,1)}, u32[]{:S(2)}, u32[]{:S(2)}) collective-permute-start(bf16[2,128,512]{2,1,0:T(8,128)(2,1)S(1)} %collective-permute-done.8.refs_0_), channel_id=1, source_target_pairs={{0,17},{1,16},{8,25},{9,24},{16,1},{17,0},{24,9},{25,8},{2,19},{3,... | collective-permute-start | bytes 786440 | tf_op jit(solution)/shard_map/ppermute | solution.py:323
  34.4 16.2 %collective-permute-start.18 = (bf16[2,128,512]{2,1,0:T(8,128)(2,1)S(1)}, bf16[2,128,512]{2,1,0:T(8,128)(2,1)}, u32[]{:S(2)}, u32[]{:S(2)}) collective-permute-start(bf16[2,128,512]{2,1,0:T(8,128)(2,1)S(1)} %collective-permute-done.16.refs_8_), channel_id=1, source_target_pairs={{0,1},{1,0},{8,9},{9,8},{16,17},{17,16},{24,25},{25,24},{2,3},{3,2... | collective-permute-start | bytes 786440 | tf_op jit(solution)/shard_map/ppermute | solution.py:323
  35.9 15.8 %collective-permute-start.20 = (bf16[2,128,512]{2,1,0:T(8,128)(2,1)S(1)}, bf16[2,128,512]{2,1,0:T(8,128)(2,1)}, u32[]{:S(2)}, u32[]{:S(2)}) collective-permute-start(bf16[2,128,512]{2,1,0:T(8,128)(2,1)S(1)} %collective-permute-done.16.refs_8_), channel_id=1, source_target_pairs={{0,16},{1,17},{8,24},{9,25},{16,0},{17,1},{24,8},{25,9},{2,18},{3,... | collective-permute-start | bytes 786440 | tf_op jit(solution)/shard_map/ppermute | solution.py:323
  40.0 13.4 %collective-permute-start.17 = (bf16[2,128,512]{2,1,0:T(8,128)(2,1)S(1)}, bf16[2,128,512]{2,1,0:T(8,128)(2,1)S(1)}, u32[]{:S(2)}, u32[]{:S(2)}) collective-permute-start(bf16[2,128,512]{2,1,0:T(8,128)(2,1)S(1)} %collective-permute-done.16.refs_8_), channel_id=1, source_target_pairs={{0,8},{1,9},{8,0},{9,1},{16,24},{17,25},{24,16},{25,17},{2,10},{3,... | collective-permute-start | bytes 786440 | tf_op jit(solution)/shard_map/ppermute | solution.py:323
  47.2 6.9 %collective-permute-start.9 = (bf16[2,128,512]{2,1,0:T(8,128)(2,1)S(1)}, bf16[2,128,512]{2,1,0:T(8,128)(2,1)S(1)}, u32[]{:S(2)}, u32[]{:S(2)}) collective-permute-start(bf16[2,128,512]{2,1,0:T(8,128)(2,1)S(1)} %collective-permute-done.8.refs_0_), channel_id=1, source_target_pairs={{0,8},{1,9},{8,0},{9,1},{16,24},{17,25},{24,16},{25,17},{2,10},{3,... | collective-permute-start | bytes 786440 | tf_op jit(solution)/shard_map/ppermute | solution.py:323
  47.2 7.0 %collective-permute-start.3 = (bf16[2,128,512]{2,1,0:T(8,128)(2,1)S(1)}, bf16[2,128,512]{2,1,0:T(8,128)(2,1)S(1)}, u32[]{:S(2)}, u32[]{:S(2)}) collective-permute-start(bf16[2,128,512]{2,1,0:T(8,128)(2,1)S(1)} %collective-permute-done.2.refs_2_), channel_id=1, source_target_pairs={{0,8},{1,9},{8,0},{9,1},{16,24},{17,25},{24,16},{25,17},{2,10},{3,... | collective-permute-start | bytes 786440 | tf_op jit(solution)/shard_map/ppermute | solution.py:323
  53.5 16.4 %collective-permute-start.11 = (bf16[2,128,512]{2,1,0:T(8,128)(2,1)S(1)}, bf16[2,128,512]{2,1,0:T(8,128)(2,1)}, u32[]{:S(2)}, u32[]{:S(2)}) collective-permute-start(bf16[2,128,512]{2,1,0:T(8,128)(2,1)S(1)} %collective-permute-done.10.refs_2_), channel_id=1, source_target_pairs={{0,8},{1,9},{8,0},{9,1},{16,24},{17,25},{24,16},{25,17},{2,10},{3,... | collective-permute-start | bytes 786440 | tf_op jit(solution)/shard_map/ppermute | solution.py:323
  54.0 15.8 %collective-permute-start.13 = (bf16[2,128,512]{2,1,0:T(8,128)(2,1)S(1)}, bf16[2,128,512]{2,1,0:T(8,128)(2,1)}, u32[]{:S(2)}, u32[]{:S(2)}) collective-permute-start(bf16[2,128,512]{2,1,0:T(8,128)(2,1)S(1)} %collective-permute-done.12.refs_4_), channel_id=1, source_target_pairs={{0,8},{1,9},{8,0},{9,1},{16,24},{17,25},{24,16},{25,17},{2,10},{3,... | collective-permute-start | bytes 786440 | tf_op jit(solution)/shard_map/ppermute | solution.py:323
  54.1 15.7 %collective-permute-start.15 = (bf16[2,128,512]{2,1,0:T(8,128)(2,1)}, bf16[2,128,512]{2,1,0:T(8,128)(2,1)}, u32[]{:S(2)}, u32[]{:S(2)}) collective-permute-start(bf16[2,128,512]{2,1,0:T(8,128)(2,1)} %collective-permute-done.14.refs_6_), channel_id=1, source_target_pairs={{0,8},{1,9},{8,0},{9,1},{16,24},{17,25},{24,16},{25,17},{2,10},{3,... | collective-permute-start | bytes 786440 | tf_op jit(solution)/shard_map/ppermute | solution.py:323
  54.6 15.3 %collective-permute-start.19 = (bf16[2,128,512]{2,1,0:T(8,128)(2,1)}, bf16[2,128,512]{2,1,0:T(8,128)(2,1)}, u32[]{:S(2)}, u32[]{:S(2)}) collective-permute-start(bf16[2,128,512]{2,1,0:T(8,128)(2,1)} %collective-permute-done.18.refs_10_), channel_id=1, source_target_pairs={{0,8},{1,9},{8,0},{9,1},{16,24},{17,25},{24,16},{25,17},{2,10},{3,... | collective-permute-start | bytes 786440 | tf_op jit(solution)/shard_map/ppermute | solution.py:323
  54.7 15.2 %collective-permute-start.21 = (bf16[2,128,512]{2,1,0:T(8,128)(2,1)}, bf16[2,128,512]{2,1,0:T(8,128)(2,1)}, u32[]{:S(2)}, u32[]{:S(2)}) collective-permute-start(bf16[2,128,512]{2,1,0:T(8,128)(2,1)} %collective-permute-done.20.refs_12_), channel_id=1, source_target_pairs={{0,8},{1,9},{8,0},{9,1},{16,24},{17,25},{24,16},{25,17},{2,10},{3,... | collective-permute-start | bytes 786440 | tf_op jit(solution)/shard_map/ppermute | solution.py:323
  86.9 5.3 %collective-permute-start.25 = (bf16[160,256]{1,0:T(8,128)(2,1)S(1)}, bf16[160,256]{1,0:T(8,128)(2,1)S(1)}, u32[]{:S(2)}, u32[]{:S(2)}) collective-permute-start(bf16[160,256]{1,0:T(8,128)(2,1)S(1)} %get-tuple-element.14), channel_id=1, source_target_pairs={{0,1},{1,0},{8,9},{9,8},{16,17},{17,16},{24,25},{25,24},{2,3},{3,2... | collective-permute-start | bytes 245768 | tf_op jit(solution)/shard_map/ppermute | solution.py:323
  87.7 5.9 %collective-permute-start.26 = (bf16[160,256]{1,0:T(8,128)(2,1)S(1)}, bf16[160,256]{1,0:T(8,128)(2,1)S(1)}, u32[]{:S(2)}, u32[]{:S(2)}) collective-permute-start(bf16[160,256]{1,0:T(8,128)(2,1)S(1)} %get-tuple-element.14), channel_id=1, source_target_pairs={{0,16},{1,17},{8,24},{9,25},{16,0},{17,1},{24,8},{25,9},{2,18},{3,... | collective-permute-start | bytes 245768 | tf_op jit(solution)/shard_map/ppermute | solution.py:323
  89.2 5.8 %collective-permute-start.27 = (bf16[160,256]{1,0:T(8,128)(2,1)S(1)}, bf16[160,256]{1,0:T(8,128)(2,1)S(1)}, u32[]{:S(2)}, u32[]{:S(2)}) collective-permute-start(bf16[160,256]{1,0:T(8,128)(2,1)S(1)} %get-tuple-element.14), channel_id=1, source_target_pairs={{0,17},{1,16},{8,25},{9,24},{16,1},{17,0},{24,9},{25,8},{2,19},{3,... | collective-permute-start | bytes 245768 | tf_op jit(solution)/shard_map/ppermute | solution.py:323
  95.1 12.9 %collective-permute-start.28 = (f32[160,256]{1,0:T(8,128)S(1)}, f32[160,256]{1,0:T(8,128)S(1)}, u32[]{:S(2)}, u32[]{:S(2)}) collective-permute-start(f32[160,256]{1,0:T(8,128)S(1)} %convert_add_fusion.keep_ref), channel_id=1, source_target_pairs={{0,8},{1,9},{8,0},{9,1},{16,24},{17,25},{24,16},{25,17},{2,10},{3,... | collective-permute-start | bytes 491528 | tf_op jit(solution)/shard_map/ppermute | solution.py:323
  95.2 11.6 %collective-permute-start.29 = (f32[100,128]{1,0:T(8,128)S(1)}, f32[100,128]{1,0:T(8,128)S(1)}, u32[]{:S(2)}, u32[]{:S(2)}) collective-permute-start(f32[100,128]{1,0:T(8,128)S(1)} %pad_maximum_fusion.2.refs_0_), channel_id=1, source_target_pairs={{0,2},{2,4},{4,6},{6,0},{1,3},{3,5},{5,7},{7,1},{8,10},{10,12},{12... | collective-permute-start | bytes 153608 | tf_op jit(solution)/shard_map/ppermute | solution.py:314
  101.3 5.4 %collective-permute-start.30 = (f32[100,128]{1,0:T(8,128)S(1)}, f32[100,128]{1,0:T(8,128)S(1)}, u32[]{:S(2)}, u32[]{:S(2)}) collective-permute-start(f32[100,128]{1,0:T(8,128)S(1)} %pad_maximum_fusion.2.refs_0_), channel_id=1, source_target_pairs={{0,4},{2,6},{4,0},{6,2},{1,5},{3,7},{5,1},{7,3},{8,12},{10,14},{12... | collective-permute-start | bytes 153608 | tf_op jit(solution)/shard_map/ppermute | solution.py:314
  103.3 4.6 %collective-permute-start.31 = (f32[100,128]{1,0:T(8,128)S(1)}, f32[100,128]{1,0:T(8,128)S(1)}, u32[]{:S(2)}, u32[]{:S(2)}) collective-permute-start(f32[100,128]{1,0:T(8,128)S(1)} %pad_maximum_fusion.2.refs_0_), channel_id=1, source_target_pairs={{0,6},{2,0},{4,2},{6,4},{1,7},{3,1},{5,3},{7,5},{8,14},{10,8},{12,... | collective-permute-start | bytes 153608 | tf_op jit(solution)/shard_map/ppermute | solution.py:314
  112.4 5.8 %collective-permute-start.32 = (f32[40,128]{1,0:T(8,128)}, f32[40,128]{1,0:T(8,128)S(1)}, u32[]{:S(2)}, u32[]{:S(2)}) collective-permute-start(f32[40,128]{1,0:T(8,128)} %get-tuple-element.9), channel_id=1, source_target_pairs={{0,6},{2,0},{4,2},{6,4},{1,7},{3,1},{5,3},{7,5},{8,14},{10,8},{12,... | collective-permute-start | bytes 61448 | tf_op jit(solution)/shard_map/ppermute | solution.py:314
  116.6 4.9 %collective-permute-start.33 = (f32[40,128]{1,0:T(8,128)}, f32[40,128]{1,0:T(8,128)S(1)}, u32[]{:S(2)}, u32[]{:S(2)}) collective-permute-start(f32[40,128]{1,0:T(8,128)} %get-tuple-element.10), channel_id=1, source_target_pairs={{0,4},{2,6},{4,0},{6,2},{1,5},{3,7},{5,1},{7,3},{8,12},{10,14},{12... | collective-permute-start | bytes 61448 | tf_op jit(solution)/shard_map/ppermute | solution.py:314
  116.6 5.8 %collective-permute-start.34 = (f32[40,128]{1,0:T(8,128)}, f32[40,128]{1,0:T(8,128)S(1)}, u32[]{:S(2)}, u32[]{:S(2)}) collective-permute-start(f32[40,128]{1,0:T(8,128)} %get-tuple-element.11), channel_id=1, source_target_pairs={{0,2},{2,4},{4,6},{6,0},{1,3},{3,5},{5,7},{7,1},{8,10},{10,12},{12... | collective-permute-start | bytes 61448 | tf_op jit(solution)/shard_map/ppermute | solution.py:314
  (34 other events, 513.8 us)
